TPU v7x, 32 devices: a whole 2x2x4 slice. The times are simulated.
32 devices in a mesh: row: 8 (over z, y), col: 4 (over x, core).
Axes of the slice: x: 2, y: 2, z: 4, core: 2. Of those that a mesh axis runs over, the one named last changes fastest.
Arguments:
- noise: float32 [8192, 512], P(('row', 'col')), may hold values from -40 to 40
- data: float32 [8192, 512], P(('col', 'row')), may hold values from -6 to 6
Outputs:
- noise_target: float32 [8192, 512], P(('row', 'col'))
- data_target: float32 [8192, 512], P(('col', 'row'))
- f_potential: float32 [8192], P('row')
- g_potential: float32 [8192], P('col')
All inputs are finite; a program needn't handle non-finite values.
Results may differ from a plain program's by a relative error of at most 0.0003.
Values sent between devices are 32-bit elements; how exact they have to be, the bound alone decides.
A program may use at most 64 MiB of HBM per device.

v0:
```python
import jax
import jax.numpy as jnp
from jax import lax
from jax.sharding import PartitionSpec as P

ITERS = 2
EPSILON = 32.0


def row_stats(scores):
    peak = lax.pmax(jnp.max(scores, axis=1), "col")
    total = lax.psum(jnp.sum(jnp.exp(scores - peak[:, None]), axis=1), "col")
    return (peak, total)


def col_stats(scores):
    peak = lax.pmax(jnp.max(scores, axis=0), "row")
    total = lax.psum(jnp.sum(jnp.exp(scores - peak[None, :]), axis=0), "row")
    return (peak, total)


def shards(noise, data):
    x_full = lax.all_gather(noise, "col", axis=0, tiled=True)
    y_full = lax.all_gather(data, "row", axis=0, tiled=True)
    x_norm = jnp.sum(x_full * x_full, axis=1)
    y_norm = jnp.sum(y_full * y_full, axis=1)
    inner = jnp.dot(
        x_full, y_full.T, precision=lax.Precision.HIGHEST, preferred_element_type=jnp.float32
    )
    cost = x_norm[:, None] + y_norm[None, :] - 2.0 * inner
    g_now = jnp.zeros((cost.shape[1],), jnp.float32)
    f_now = jnp.zeros((cost.shape[0],), jnp.float32)
    col_scores = cost
    col_peak = g_now
    col_total = g_now
    for step in range(ITERS):
        row_scores = (g_now[None, :] - cost) / EPSILON
        peak, total = row_stats(row_scores)
        f_now = -EPSILON * (peak + jnp.log(total))
        col_scores = (f_now[:, None] - cost) / EPSILON
        col_peak, col_total = col_stats(col_scores)
        g_now = -EPSILON * (col_peak + jnp.log(col_total))
    col_weights = jnp.exp(col_scores - col_peak[None, :]) / col_total[None, :]
    data_part = jnp.dot(
        col_weights.T, x_full, precision=lax.Precision.HIGHEST, preferred_element_type=jnp.float32
    )
    data_target = lax.psum_scatter(data_part, "row", scatter_dimension=0, tiled=True)
    final_scores = (g_now[None, :] - cost) / EPSILON
    peak, total = row_stats(final_scores)
    weights = jnp.exp(final_scores - peak[:, None]) / total[:, None]
    noise_part = jnp.dot(
        weights, y_full, precision=lax.Precision.HIGHEST, preferred_element_type=jnp.float32
    )
    noise_target = lax.psum_scatter(noise_part, "col", scatter_dimension=0, tiled=True)
    return (noise_target, data_target, f_now, g_now)


def solution(mesh):
    placed = (P(("row", "col"), None), P(("col", "row"), None))
    return jax.shard_map(
        shards,
        mesh=mesh,
        in_specs=placed,
        out_specs=(P(("row", "col"), None), P(("col", "row"), None), P("row"), P("col")),
        check_vma=False,
    )
```

profile of v0, /device:TPU:0, one launch (start us, length us, event | category | flops | bytes accessed | tf_op | source)
XLA Modules:
  0.0 431.4 jit_solution(6373098548882051552)
XLA Ops:
  7.2 0.0 all-gather.3.cloned.1.call-start
  7.2 0.7 all-gather.3.cloned.1.call-update
  7.9 0.0 all-gather.5.cloned.1.call-start
  7.9 0.7 all-gather.5.cloned.1.call-update
  8.6 0.0 reduce-scatter.3.cloned.1.call-start
  8.7 26.2 %all-gather.3.cloned.1.call-done = f32[1024,512]{1,0:T(8,128)} async-done(((f32[256,512]{1,0:T(8,128)}), f32[1024,512]{1,0:T(8,128)}) %all-gather.3.cloned.1.call-update) | async-done | bytes 2097168 | tf_op jit(solution)/shard_map/all_gather | solution.py:23
  34.8 1.8 multiply_reduce_fusion.1
  36.7 73.1 %all-gather.5.cloned.1.call-done = f32[2048,512]{1,0:T(8,128)} async-done(((f32[256,512]{1,0:T(8,128)}), f32[2048,512]{1,0:T(8,128)}) %all-gather.5.cloned.1.call-update) | async-done | bytes 4194320 | tf_op jit(solution)/shard_map/all_gather | solution.py:24
  109.8 2.5 multiply_reduce_fusion
  112.3 18.8 %fusion.4 = (f32[1024]{0:T(1024)S(1)}, f32[1024,2048]{1,0:T(8,128)}) fusion(f32[1024,512]{1,0:T(8,128)} %all-gather.3.cloned.1.call-done, f32[2048,512]{1,0:T(8,128)} %all-gather.5.cloned.1.call-done, f32[2048]{0:T(1024)S(1)} %multiply_reduce_fusion, f32[1024]{0:T(1024)S(1)} %multiply_reduce_fusion.1), kind=kOutput, calls=%fused_computation.15 | convolution fusion | flops 12897483776 | bytes 14696448 | tf_op jit(solution)/shard_map/dot_general | solution.py:27
  131.1 5.6 %pmax.35 = f32[1024]{0:T(1024)S(1)} all-reduce(f32[1024]{0:T(1024)S(1)} %get-tuple-element.4), channel_id=1, replica_groups=mesh['row'=8,'col'=4] {'col'}, use_global_device_ids=true, to_apply=%region_3.0 | all-reduce | flops 1024 | bytes 8192 | tf_op jit(solution)/shard_map/pmax | solution.py:11
  136.7 4.5 %exponential_reduce_fusion.2 = f32[1024]{0:T(1024)S(1)} fusion(f32[1024,2048]{1,0:T(8,128)} %get-tuple-element.5, f32[1024]{0:T(1024)S(1)} %pmax.35), kind=kLoop, calls=%fused_computation.12 | loop fusion | flops 8387584 | bytes 8396800 | tf_op jit(solution)/shard_map/reduce_sum | solution.py:12
  141.2 6.6 %psum.35 = f32[1024]{0:T(1024)S(1)} all-reduce(f32[1024]{0:T(1024)S(1)} %exponential_reduce_fusion.2), channel_id=1, replica_groups=mesh['row'=8,'col'=4] {'col'}, use_global_device_ids=true, to_apply=%region_5.0 | all-reduce | flops 1024 | bytes 8192 | tf_op jit(solution)/shard_map/psum | solution.py:12
  147.8 4.3 fusion.5
  152.1 19.2 %pmax.36 = f32[2048]{0:T(1024)S(1)} all-reduce(f32[2048]{0:T(1024)S(1)} %fusion.5), channel_id=1, replica_groups=mesh['row'=8,'col'=4] {'row'}, use_global_device_ids=true, to_apply=%region_7.0 | all-reduce | flops 2048 | bytes 16384 | tf_op jit(solution)/shard_map/pmax | solution.py:17
  171.4 4.5 %exponential_reduce_fusion.1 = f32[2048]{0:T(1024)S(1)} fusion(f32[1024,2048]{1,0:T(8,128)} %get-tuple-element.5, f32[2048]{0:T(1024)S(1)} %pmax.36, f32[1024]{0:T(1024)S(1)} %add_multiply_fusion.3), kind=kLoop, calls=%fused_computation.10 | loop fusion | flops 8386560 | bytes 8409088 | tf_op jit(solution)/shard_map/reduce_sum | solution.py:18
  175.9 17.7 %psum.36 = f32[2048]{0:T(1024)S(1)} all-reduce(f32[2048]{0:T(1024)S(1)} %exponential_reduce_fusion.1), channel_id=1, replica_groups=mesh['row'=8,'col'=4] {'row'}, use_global_device_ids=true, to_apply=%region_9.0 | all-reduce | flops 2048 | bytes 16384 | tf_op jit(solution)/shard_map/psum | solution.py:18
  193.6 4.3 fusion.6
  197.9 5.7 %pmax.37 = f32[1024]{0:T(1024)S(1)} all-reduce(f32[1024]{0:T(1024)S(1)} %fusion.6), channel_id=1, replica_groups=mesh['row'=8,'col'=4] {'col'}, use_global_device_ids=true, to_apply=%region_11.0 | all-reduce | flops 1024 | bytes 8192 | tf_op jit(solution)/shard_map/pmax | solution.py:11
  203.6 4.5 %exponential_reduce_fusion = f32[1024]{0:T(1024)S(1)} fusion(f32[1024,2048]{1,0:T(8,128)} %get-tuple-element.5, f32[1024]{0:T(1024)S(1)} %pmax.37, f32[2048]{0:T(1024)S(1)} %add_multiply_fusion.1), kind=kLoop, calls=%fused_computation.8 | loop fusion | flops 8387584 | bytes 8404992 | tf_op jit(solution)/shard_map/reduce_sum | solution.py:12
  208.1 6.3 %psum.37 = f32[1024]{0:T(1024)S(1)} all-reduce(f32[1024]{0:T(1024)S(1)} %exponential_reduce_fusion), channel_id=1, replica_groups=mesh['row'=8,'col'=4] {'col'}, use_global_device_ids=true, to_apply=%region_13.0 | all-reduce | flops 1024 | bytes 8192 | tf_op jit(solution)/shard_map/psum | solution.py:12
  214.4 0.0 copy-start.2
  214.4 4.3 fusion.7
  218.6 19.1 %pmax.38 = f32[2048]{0:T(1024)S(1)} all-reduce(f32[2048]{0:T(1024)S(1)} %fusion.7), channel_id=1, replica_groups=mesh['row'=8,'col'=4] {'row'}, use_global_device_ids=true, to_apply=%region_15.0 | all-reduce | flops 2048 | bytes 16384 | tf_op jit(solution)/shard_map/pmax | solution.py:17
  237.8 4.5 %fusion.9 = f32[2048]{0:T(1024)S(1)} fusion(f32[1024,2048]{1,0:T(8,128)} %get-tuple-element.5, f32[2048]{0:T(1024)S(1)} %pmax.38, f32[1024]{0:T(1024)S(1)} %add_multiply_fusion.2), kind=kLoop, calls=%fused_computation.20 | loop fusion | flops 8386560 | bytes 8409088 | tf_op jit(solution)/shard_map/reduce_sum | solution.py:18
  242.3 17.7 %psum.38 = f32[2048]{0:T(1024)S(1)} all-reduce(f32[2048]{0:T(1024)S(1)} %fusion.9), channel_id=1, replica_groups=mesh['row'=8,'col'=4] {'row'}, use_global_device_ids=true, to_apply=%region_17.0 | all-reduce | flops 2048 | bytes 16384 | tf_op jit(solution)/shard_map/psum | solution.py:18
  260.0 0.0 copy-start.1
  260.0 4.3 fusion.8
  264.3 5.7 %pmax.39 = f32[1024]{0:T(1024)S(1)} all-reduce(f32[1024]{0:T(1024)S(1)} %fusion.8), channel_id=1, replica_groups=mesh['row'=8,'col'=4] {'col'}, use_global_device_ids=true, to_apply=%region_19.0 | all-reduce | flops 1024 | bytes 8192 | tf_op jit(solution)/shard_map/pmax | solution.py:11
  270.0 4.5 %fusion.10 = f32[1024]{0:T(1024)S(1)} fusion(f32[1024,2048]{1,0:T(8,128)} %get-tuple-element.5, f32[1024]{0:T(1024)S(1)} %pmax.39, f32[2048]{0:T(1024)S(1)} %add_multiply_fusion), kind=kLoop, calls=%fused_computation.21 | loop fusion | flops 8387584 | bytes 8404992 | tf_op jit(solution)/shard_map/reduce_sum | solution.py:12
  274.4 6.5 %psum.39 = f32[1024]{0:T(1024)S(1)} all-reduce(f32[1024]{0:T(1024)S(1)} %fusion.10), channel_id=1, replica_groups=mesh['row'=8,'col'=4] {'col'}, use_global_device_ids=true, to_apply=%region_21.0 | all-reduce | flops 1024 | bytes 8192 | tf_op jit(solution)/shard_map/psum | solution.py:12
  281.0 0.0 copy-done.1
  281.0 0.0 copy-start
  281.0 22.4 %fusion.2 = f32[1024,512]{1,0:T(8,128)} fusion(f32[2048,512]{1,0:T(8,128)} %all-gather.5.cloned.1.call-done, f32[1024,2048]{1,0:T(8,128)} %get-tuple-element.5, f32[1024]{0:T(1024)S(1)} %psum.39, f32[1024]{0:T(1024)S(1)} %pmax.39, f32[2048]{0:T(1024)S(1)} %add_multiply_fusion), kind=kOutput, calls=%fused_computation.2 | convolution fusion | flops 12893290496 | bytes 14696448 | tf_op jit(solution)/shard_map/dot_general | solution.py:51
  303.4 0.0 reduce-scatter.3.cloned.1.call-update
  303.4 0.3 reduce-scatter.5.cloned.1.call-start
  303.7 0.0 copy-done.2
  303.7 0.0 copy-done
  303.7 18.5 %fusion = f32[2048,512]{1,0:T(8,128)} fusion(f32[1024,512]{1,0:T(8,128)S(1)} %copy-done, f32[1024,2048]{1,0:T(8,128)} %get-tuple-element.5, f32[2048]{0:T(1024)S(1)} %psum.38, f32[2048]{0:T(1024)S(1)} %pmax.38, f32[1024]{0:T(1024)S(1)} %add_multiply_fusion.2), kind=kOutput, calls=%fused_computation | convolution fusion | flops 12893290496 | bytes 14700544 | tf_op jit(solution)/shard_map/dot_general | solution.py:44
  322.2 0.0 reduce-scatter.5.cloned.1.call-update
  322.3 10.3 %reduce-scatter.3.cloned.1.call-done = f32[256,512]{1,0:T(8,128)} async-done(((f32[1024,512]{1,0:T(8,128)}), f32[256,512]{1,0:T(8,128)}) %reduce-scatter.3.cloned.1.call-update) | async-done | bytes 524304 | tf_op jit(solution)/shard_map/reduce_scatter | solution.py:54
  332.5 92.4 %reduce-scatter.5.cloned.1.call-done = f32[256,512]{1,0:T(8,128)} async-done(((f32[2048,512]{1,0:T(8,128)}), f32[256,512]{1,0:T(8,128)}) %reduce-scatter.5.cloned.1.call-update) | async-done | bytes 524304 | tf_op jit(solution)/shard_map/reduce_scatter | solution.py:47
  (4 shorter events, 0.0 us)
Async XLA Ops:
  7.2 27.7 %all-gather.3.cloned.1.call-start = ((), (), s32[]{:S(2)}) async-start(), calls=%async_computation.2 | async-start | bytes 2621440 | tf_op jit(solution)/shard_map/all_gather | solution.py:23
  7.9 101.9 %all-gather.5.cloned.1.call-start = ((), (), s32[]{:S(2)}) async-start(), calls=%async_computation.3 | async-start | bytes 4718592 | tf_op jit(solution)/shard_map/all_gather | solution.py:24
  8.6 323.9 %reduce-scatter.3.cloned.1.call-start = ((), (), s32[]{:S(2)}) async-start(), calls=%async_computation.4 | async-start | bytes 2621440 | tf_op jit(solution)/shard_map/reduce_scatter | solution.py:54
  214.4 89.3 %copy-start.2 = (f32[1024]{0:T(1024)}, f32[1024]{0:T(1024)S(1)}, u32[]{:S(2)}) copy-start(f32[1024]{0:T(1024)S(1)} %add_multiply_fusion.2) | copy-start | bytes 12292
  260.0 21.0 %copy-start.1 = (f32[2048]{0:T(1024)}, f32[2048]{0:T(1024)S(1)}, u32[]{:S(2)}) copy-start(f32[2048]{0:T(1024)S(1)} %add_multiply_fusion) | copy-start | bytes 24580
  281.0 22.7 %copy-start = (f32[1024,512]{1,0:T(8,128)S(1)}, f32[1024,512]{1,0:T(8,128)}, u32[]{:S(2)}) copy-start(f32[1024,512]{1,0:T(8,128)} %all-gather.3.cloned.1.call-done) | copy-start | bytes 6291460
  303.4 121.5 %reduce-scatter.5.cloned.1.call-start = ((), (), s32[]{:S(2)}) async-start(), calls=%async_computation.5 | async-start | bytes 4718592 | tf_op jit(solution)/shard_map/reduce_scatter | solution.py:47
Sparse Core Ops, SparseCore 0:
  9.5 25.2 all-gather.2
  37.0 72.7 all-gather.4
  303.5 28.9 reduce-scatter.2
  336.6 88.2 reduce-scatter.4
where the time goes:
time: 432 us; the launch traced here: 431 us
  waiting for transfers between devices  203 us (47%)
  blocking collectives  110 us (25%)
  matrix products  59.7 us (14%)
  other arithmetic  43.9 us (10%)
  between operations  13.9 us (3%)
    reduce_scatter x1, waiting for transfers between devices, shards(): lax.psum_scatter(data_part, 'row', scatter_dimension=0, tiled=True)  92.4 us
    all_gather x1, waiting for transfers between devices, shards(): y_full = lax.all_gather(data, 'row', axis=0, tiled=True)  73.1 us
    pmax x2, blocking collectives, col_stats(): peak = lax.pmax(jnp.max(scores, axis=0), 'row')  38.4 us
    psum x2, blocking collectives, col_stats(): total = lax.psum(jnp.sum(jnp.exp(scores - peak[None, :]), axis=0), 'row')  35.4 us
    all_gather x1, waiting for transfers between devices, shards(): x_full = lax.all_gather(noise, 'col', axis=0, tiled=True)  26.2 us
    dot_general x1, matrix products, shards(): jnp.dot(weights, y_full, precision=lax.Precision.HIGHEST, preferred_eleme...  22.4 us
    psum x3, blocking collectives, row_stats(): total = lax.psum(jnp.sum(jnp.exp(scores - peak[:, None]), axis=1), 'col')  19.4 us
    dot_general x1, matrix products, shards(): jnp.dot(x_full, y_full.T, precision=lax.Precision.HIGHEST, preferred_elem...  18.8 us
  transfers between devices with their start and end apart: 4, of which 4 were waited for; matrix products, arithmetic and copies ran while one was open for 5% of the time, Pallas kernels for 0%

commit v1 on v0

--- a/solution.py
+++ b/solution.py
@@ -1,10 +1,20 @@
+import functools
 import jax
 import jax.numpy as jnp
 from jax import lax
 from jax.sharding import PartitionSpec as P
+from jax.lax import all_gather
 
 ITERS = 2
 EPSILON = 32.0
+
+
+def pair_the_rates(in_array, axis_key):
+    top = all_gather(in_array, axis_key)
+    return jnp.sum(top, axis=0)
+
+
+_enter_cells = functools.partial(pair_the_rates, axis_key="row")
 
 
 def row_stats(scores):
@@ -15,7 +25,7 @@
 
 def col_stats(scores):
     peak = lax.pmax(jnp.max(scores, axis=0), "row")
-    total = lax.psum(jnp.sum(jnp.exp(scores - peak[None, :]), axis=0), "row")
+    total = _enter_cells(jnp.sum(jnp.exp(scores - peak[None, :]), axis=0))
     return (peak, total)
 
 

time: 432 us -> 456 us (1.056)
  blocking collectives: 110 us -> 134 us
    all_gather x0 -> x2, blocking collectives: none -> 61.3 us  [pair_the_rates(): top = all_gather(in_array, axis_key)]
    psum x2 -> x0, blocking collectives: 35.4 us -> none  [col_stats(): total = lax.psum(jnp.sum(jnp.exp(scores - peak[None, :]), axis=0), 'row')]
  transfers between devices with their start and end apart: 4 -> 4, of which waited for: 4 -> 4; matrix products, arithmetic and copies ran while one was open for 5% -> 4% of each run, Pallas kernels for 0% -> 0%
where the time goes in v1:
time: 456 us
  waiting for transfers between devices  203 us (45%)
  blocking collectives  134 us (29%)
  matrix products  59.7 us (13%)
  other arithmetic  44 us (10%)
  between operations  13.9 us (3%)
    reduce_scatter x1, waiting for transfers between devices, shards(): lax.psum_scatter(data_part, 'row', scatter_dimension=0, tiled=True)  92.4 us
    all_gather x1, waiting for transfers between devices, shards(): y_full = lax.all_gather(data, 'row', axis=0, tiled=True)  73.1 us
    all_gather x2, blocking collectives, pair_the_rates(): top = all_gather(in_array, axis_key)  61.3 us
    pmax x2, blocking collectives, col_stats(): peak = lax.pmax(jnp.max(scores, axis=0), 'row')  36.9 us
    all_gather x1, waiting for transfers between devices, shards(): x_full = lax.all_gather(noise, 'col', axis=0, tiled=True)  26.2 us
    dot_general x1, matrix products, shards(): jnp.dot(weights, y_full, precision=lax.Precision.HIGHEST, preferred_eleme...  22.4 us
    psum x3, blocking collectives, row_stats(): total = lax.psum(jnp.sum(jnp.exp(scores - peak[:, None]), axis=1), 'col')  19.3 us
    dot_general x1, matrix products, shards(): jnp.dot(x_full, y_full.T, precision=lax.Precision.HIGHEST, preferred_elem...  18.8 us
  transfers between devices with their start and end apart: 4, of which 4 were waited for; matrix products, arithmetic and copies ran while one was open for 4% of the time, Pallas kernels for 0%

profile of v1, /device:TPU:0, one launch (start us, length us, event | category | flops | bytes accessed | tf_op | source)
XLA Modules:
  0.0 455.9 jit_solution(15734581166364021045)
XLA Ops:
  7.2 0.0 all-gather.5.cloned.1.call-start
  7.2 0.7 all-gather.5.cloned.1.call-update
  7.9 0.0 all-gather.7.cloned.1.call-start
  7.9 0.7 all-gather.7.cloned.1.call-update
  8.6 0.0 reduce-scatter.3.cloned.1.call-start
  8.7 26.2 %all-gather.5.cloned.1.call-done = f32[1024,512]{1,0:T(8,128)} async-done(((f32[256,512]{1,0:T(8,128)}), f32[1024,512]{1,0:T(8,128)}) %all-gather.5.cloned.1.call-update) | async-done | bytes 2097168 | tf_op jit(solution)/shard_map/all_gather | solution.py:33
  34.8 1.8 multiply_reduce_fusion.1
  36.7 73.1 %all-gather.7.cloned.1.call-done = f32[2048,512]{1,0:T(8,128)} async-done(((f32[256,512]{1,0:T(8,128)}), f32[2048,512]{1,0:T(8,128)}) %all-gather.7.cloned.1.call-update) | async-done | bytes 4194320 | tf_op jit(solution)/shard_map/all_gather | solution.py:34
  109.8 2.5 multiply_reduce_fusion
  112.3 18.8 %fusion.4 = (f32[1024]{0:T(1024)S(1)}, f32[1024,2048]{1,0:T(8,128)}) fusion(f32[1024,512]{1,0:T(8,128)} %all-gather.5.cloned.1.call-done, f32[2048,512]{1,0:T(8,128)} %all-gather.7.cloned.1.call-done, f32[2048]{0:T(1024)S(1)} %multiply_reduce_fusion, f32[1024]{0:T(1024)S(1)} %multiply_reduce_fusion.1), kind=kOutput, calls=%fused_computation.15 | convolution fusion | flops 12897483776 | bytes 14696448 | tf_op jit(solution)/shard_map/dot_general | solution.py:37
  131.1 5.6 %pmax.35 = f32[1024]{0:T(1024)S(1)} all-reduce(f32[1024]{0:T(1024)S(1)} %get-tuple-element.4), channel_id=1, replica_groups=mesh['row'=8,'col'=4] {'col'}, use_global_device_ids=true, to_apply=%region_3.0 | all-reduce | flops 1024 | bytes 8192 | tf_op jit(solution)/shard_map/pmax | solution.py:21
  136.7 4.5 exponential_reduce_fusion.2
  141.2 6.6 %psum.21 = f32[1024]{0:T(1024)S(1)} all-reduce(f32[1024]{0:T(1024)S(1)} %exponential_reduce_fusion.2), channel_id=1, replica_groups=mesh['row'=8,'col'=4] {'col'}, use_global_device_ids=true, to_apply=%region_5.0 | all-reduce | flops 1024 | bytes 8192 | tf_op jit(solution)/shard_map/psum | solution.py:22
  147.8 4.3 fusion.5
  152.1 19.2 %pmax.36 = f32[2048]{0:T(1024)S(1)} all-reduce(f32[2048]{0:T(1024)S(1)} %fusion.5), channel_id=1, replica_groups=mesh['row'=8,'col'=4] {'row'}, use_global_device_ids=true, to_apply=%region_7.0 | all-reduce | flops 2048 | bytes 16384 | tf_op jit(solution)/shard_map/pmax | solution.py:27
  171.4 4.5 exponential_reduce_fusion.1
  175.9 30.7 %all-gather = f32[16384]{0:T(1024)S(1)} all-gather(f32[2048]{0:T(1024)S(1)} %exponential_reduce_fusion.1), channel_id=2, replica_groups=mesh['row'=8,'col'=4] {'row'}, dimensions={0}, use_global_device_ids=true | all-gather | bytes 73728 | tf_op jit(solution)/shard_map/all_gather | solution.py:13
  206.7 4.3 fusion.6
  210.9 5.7 %pmax.37 = f32[1024]{0:T(1024)S(1)} all-reduce(f32[1024]{0:T(1024)S(1)} %fusion.6), channel_id=1, replica_groups=mesh['row'=8,'col'=4] {'col'}, use_global_device_ids=true, to_apply=%region_11.0 | all-reduce | flops 1024 | bytes 8192 | tf_op jit(solution)/shard_map/pmax | solution.py:21
  216.6 4.5 exponential_reduce_fusion
  221.1 6.2 %psum.22 = f32[1024]{0:T(1024)S(1)} all-reduce(f32[1024]{0:T(1024)S(1)} %exponential_reduce_fusion), channel_id=1, replica_groups=mesh['row'=8,'col'=4] {'col'}, use_global_device_ids=true, to_apply=%region_13.0 | all-reduce | flops 1024 | bytes 8192 | tf_op jit(solution)/shard_map/psum | solution.py:22
  227.3 0.0 copy-start.2
  227.3 4.3 fusion.7
  231.6 17.6 %pmax.38 = f32[2048]{0:T(1024)S(1)} all-reduce(f32[2048]{0:T(1024)S(1)} %fusion.7), channel_id=1, replica_groups=mesh['row'=8,'col'=4] {'row'}, use_global_device_ids=true, to_apply=%region_15.0 | all-reduce | flops 2048 | bytes 16384 | tf_op jit(solution)/shard_map/pmax | solution.py:27
  249.2 4.5 fusion.9
  253.7 30.5 %all-gather.1 = f32[16384]{0:T(1024)S(1)} all-gather(f32[2048]{0:T(1024)S(1)} %fusion.9), channel_id=3, replica_groups=mesh['row'=8,'col'=4] {'row'}, dimensions={0}, use_global_device_ids=true | all-gather | bytes 73728 | tf_op jit(solution)/shard_map/all_gather | solution.py:13
  284.3 0.0 copy-start.1
  284.4 4.3 fusion.8
  288.6 5.7 %pmax.39 = f32[1024]{0:T(1024)S(1)} all-reduce(f32[1024]{0:T(1024)S(1)} %fusion.8), channel_id=1, replica_groups=mesh['row'=8,'col'=4] {'col'}, use_global_device_ids=true, to_apply=%region_19.0 | all-reduce | flops 1024 | bytes 8192 | tf_op jit(solution)/shard_map/pmax | solution.py:21
  294.3 4.5 fusion.10
  298.8 6.5 %psum.23 = f32[1024]{0:T(1024)S(1)} all-reduce(f32[1024]{0:T(1024)S(1)} %fusion.10), channel_id=1, replica_groups=mesh['row'=8,'col'=4] {'col'}, use_global_device_ids=true, to_apply=%region_21.0 | all-reduce | flops 1024 | bytes 8192 | tf_op jit(solution)/shard_map/psum | solution.py:22
  305.3 0.0 copy-done.1
  305.3 0.0 copy-start
  305.3 22.4 %fusion.2 = f32[1024,512]{1,0:T(8,128)} fusion(f32[2048,512]{1,0:T(8,128)} %all-gather.7.cloned.1.call-done, f32[1024,2048]{1,0:T(8,128)} %get-tuple-element.5, f32[1024]{0:T(1024)S(1)} %psum.23, f32[1024]{0:T(1024)S(1)} %pmax.39, f32[2048]{0:T(1024)S(1)} %add_multiply_fusion), kind=kOutput, calls=%fused_computation.2 | convolution fusion | flops 12893290496 | bytes 14696448 | tf_op jit(solution)/shard_map/dot_general | solution.py:61
  327.7 0.0 reduce-scatter.3.cloned.1.call-update
  327.7 0.3 reduce-scatter.5.cloned.1.call-start
  328.0 0.0 copy-done.2
  328.0 0.0 copy-done
  328.0 18.5 %fusion = f32[2048,512]{1,0:T(8,128)} fusion(f32[1024,512]{1,0:T(8,128)S(1)} %copy-done, f32[1024,2048]{1,0:T(8,128)} %get-tuple-element.5, f32[2048]{0:T(1024)S(1)} %reduce_sum.88, f32[2048]{0:T(1024)S(1)} %pmax.38, f32[1024]{0:T(1024)S(1)} %add_multiply_fusion.2), kind=kOutput, calls=%fused_computation | convolution fusion | flops 12893290496 | bytes 14700544 | tf_op jit(solution)/shard_map/dot_general | solution.py:54
  346.5 0.0 reduce-scatter.5.cloned.1.call-update
  346.6 10.4 %reduce-scatter.3.cloned.1.call-done = f32[256,512]{1,0:T(8,128)} async-done(((f32[1024,512]{1,0:T(8,128)}), f32[256,512]{1,0:T(8,128)}) %reduce-scatter.3.cloned.1.call-update) | async-done | bytes 524304 | tf_op jit(solution)/shard_map/reduce_scatter | solution.py:64
  356.9 92.4 %reduce-scatter.5.cloned.1.call-done = f32[256,512]{1,0:T(8,128)} async-done(((f32[2048,512]{1,0:T(8,128)}), f32[256,512]{1,0:T(8,128)}) %reduce-scatter.5.cloned.1.call-update) | async-done | bytes 524304 | tf_op jit(solution)/shard_map/reduce_scatter | solution.py:57
  (8 shorter events, 0.1 us)
Async XLA Ops:
  7.2 27.7 %all-gather.5.cloned.1.call-start = ((), (), s32[]{:S(2)}) async-start(), calls=%async_computation.2 | async-start | bytes 2621440 | tf_op jit(solution)/shard_map/all_gather | solution.py:33
  7.9 101.9 %all-gather.7.cloned.1.call-start = ((), (), s32[]{:S(2)}) async-start(), calls=%async_computation.3 | async-start | bytes 4718592 | tf_op jit(solution)/shard_map/all_gather | solution.py:34
  8.6 348.3 %reduce-scatter.3.cloned.1.call-start = ((), (), s32[]{:S(2)}) async-start(), calls=%async_computation.4 | async-start | bytes 2621440 | tf_op jit(solution)/shard_map/reduce_scatter | solution.py:64
  227.3 100.7 %copy-start.2 = (f32[1024]{0:T(1024)}, f32[1024]{0:T(1024)S(1)}, u32[]{:S(2)}) copy-start(f32[1024]{0:T(1024)S(1)} %add_multiply_fusion.2) | copy-start | bytes 12292
  284.3 20.9 %copy-start.1 = (f32[2048]{0:T(1024)}, f32[2048]{0:T(1024)S(1)}, u32[]{:S(2)}) copy-start(f32[2048]{0:T(1024)S(1)} %add_multiply_fusion) | copy-start | bytes 24580
  305.3 22.7 %copy-start = (f32[1024,512]{1,0:T(8,128)S(1)}, f32[1024,512]{1,0:T(8,128)}, u32[]{:S(2)}) copy-start(f32[1024,512]{1,0:T(8,128)} %all-gather.5.cloned.1.call-done) | copy-start | bytes 6291460
  327.7 121.6 %reduce-scatter.5.cloned.1.call-start = ((), (), s32[]{:S(2)}) async-start(), calls=%async_computation.5 | async-start | bytes 4718592 | tf_op jit(solution)/shard_map/reduce_scatter | solution.py:57
Sparse Core Ops, SparseCore 0:
  9.5 25.2 all-gather.4
  37.0 72.7 all-gather.6
  327.9 29.0 reduce-scatter.2
  361.0 88.2 reduce-scatter.4
